TPU v7x, 16 devices: a whole 2x2x2 slice. The times are simulated.
16 devices in a mesh: dp: 1, ep: 16 (over x, y, z, core).
Axes of the slice: x: 2, y: 2, z: 2, core: 2. Of those that a mesh axis runs over, the one named last changes fastest.
Arguments:
- x: bfloat16 [1, 16, 256, 3072], P('dp', 'ep')
- expert: int32 [1, 16, 256, 4], P('dp', 'ep')
- slot: int32 [1, 16, 256, 4], P('dp', 'ep')
- gate: float32 [1, 16, 256, 4], P('dp', 'ep')
- w_gate: bfloat16 [16, 3072, 10752], P('ep')
- w_up: bfloat16 [16, 3072, 10752], P('ep')
- w_down: bfloat16 [16, 10752, 3072], P('ep')
Outputs:
- y: bfloat16 [1, 16, 256, 3072], P('dp', 'ep')
All inputs are finite; a program needn't handle non-finite values.
Results may differ from a plain program's by a relative error of at most 0.009.
Values are sent between devices in bfloat16 or wider.
A program may use at most 2 GiB of HBM per device.

v0:
```python
import jax
import jax.numpy as jnp
from jax import lax
from jax.sharding import NamedSharding, PartitionSpec as P


def einsum(form, a, b):
    return jnp.einsum(form, a.astype(jnp.float32), b.astype(jnp.float32))


def solution(mesh):
    def placed(v, *spec):
        return lax.with_sharding_constraint(v, NamedSharding(mesh, P(*spec)))

    def step(x, expert, slot, gate, w_gate, w_up, w_down):
        experts, (tokens, top) = w_gate.shape[0], expert.shape[2:]
        slots = 5 * tokens * top // (4 * experts)
        to_expert = jax.nn.one_hot(expert, experts, dtype=jnp.bfloat16)
        to_slot = jax.nn.one_hot(slot, slots, dtype=jnp.bfloat16)
        weighted = to_expert * gate[..., None].astype(jnp.bfloat16)
        dispatch = einsum("abtke,abtkc->abtec", to_expert, to_slot).astype(jnp.bfloat16)
        combine = einsum("abtke,abtkc->abtec", weighted, to_slot).astype(jnp.bfloat16)
        z = einsum("abtec,abtd->aebcd", dispatch, x).astype(jnp.bfloat16)
        z = placed(z, "dp", None, "ep", None, None)
        z = placed(z, "dp", "ep", None, None, None)
        h = jax.nn.silu(einsum("aebcd,edf->aebcf", z, w_gate))
        h = (h * einsum("aebcd,edf->aebcf", z, w_up)).astype(jnp.bfloat16)
        out = einsum("aebcf,efd->aebcd", h, w_down).astype(jnp.bfloat16)
        out = placed(out, "dp", "ep", None, None, None)
        out = placed(out, "dp", None, "ep", None, None)
        y = einsum("abtec,aebcd->abtd", combine, out)
        return y.astype(jnp.bfloat16)

    return step
```

profile of v0, /device:TPU:13, one launch (start us, length us, event | category | flops | bytes accessed | tf_op | source)
XLA Modules:
  0.0 521.2 jit_solution(2041859233611705810)
XLA Ops:
  0.0 0.0 copy-start
  0.0 0.9 copy.3
  0.9 0.0 copy-start.2
  1.0 0.8 copy.5
  1.8 0.0 copy-done.2
  1.8 0.0 copy-start.4
  1.8 0.6 copy-done.4
  2.5 2.0 fusion.35
  4.5 0.8 copy.9
  5.3 0.0 copy-done
  5.3 2.2 convert_bitcast_fusion.1
  7.5 90.8 %all-to-all.4 = bf16[1,16,1,1,80,3072]{5,4,3,2,0,1:T(8,128)(2,1)S(1)} all-to-all(bf16[1,16,1,1,80,3072]{5,4,3,2,0,1:T(8,128)(2,1)S(1)} %convert_bitcast_fusion.1), channel_id=1, replica_groups=mesh['dp'=1,'ep'=16] {'ep'}, dimensions={1} | all-to-all | bytes 15728640 | tf_op jit(solution)/sharding_constraint;jit(solution)/sharding_constraint | solution.py:13
  98.3 94.4 %fusion.2 = f32[16,80,10752]{2,1,0:T(8,128)} fusion(bf16[1,3072,10752]{2,1,0:T(8,128)(2,1)} %param.5, bf16[1,16,1,1,80,3072]{5,4,3,2,0,1:T(8,128)(2,1)S(1)} %all-to-all.4), kind=kOutput, calls=%fused_computation.2 | convolution fusion | flops 84557168640 | bytes 128974848 | tf_op jit(solution)/aebcd,edf->aebcf/dot_general | solution.py:8
  192.7 101.5 %fusion.6 = bf16[1,1,16,80,10752]{4,3,2,0,1:T(8,128)(2,1)} fusion(f32[16,80,10752]{2,1,0:T(8,128)} %fusion.2, bf16[1,3072,10752]{2,1,0:T(8,128)(2,1)} %param.4, bf16[1,16,1,1,80,3072]{5,4,3,2,0,1:T(8,128)(2,1)S(1)} %all-to-all.4), kind=kOutput, calls=%fused_computation.7 | convolution fusion | flops 84639744000 | bytes 156499968 | tf_op jit(solution)/aebcd,edf->aebcf/dot_general | solution.py:8
  294.1 0.0 copy-start.1
  294.1 95.8 %convert_bitcast_fusion = bf16[1,1,16,1,80,3072]{5,4,3,1,0,2:T(8,128)(2,1)} fusion(bf16[1,10752,3072]{2,1,0:T(8,128)(2,1)} %param.6, bf16[1,1,16,80,10752]{4,3,2,0,1:T(8,128)(2,1)} %fusion.6), kind=kOutput, calls=%fused_computation.18 | convolution fusion | flops 84561100800 | bytes 101449728 | tf_op jit(solution)/aebcf,efd->aebcd/dot_general | solution.py:8
  389.9 5.8 %all-to-all-start.1 = ((bf16[1,1,16,1,80,3072]{5,4,3,1,0,2:T(8,128)(2,1)}), bf16[1,1,16,1,80,3072]{5,4,3,1,0,2:T(8,128)(2,1)}, u32[]{:S(2)}, u32[]{:S(2)}) async-start(bf16[1,1,16,1,80,3072]{5,4,3,1,0,2:T(8,128)(2,1)} %convert_bitcast_fusion), calls=%async_computation.1 | async-start | bytes 15728640 | tf_op jit(solution)/sharding_constraint;jit(solution)/sharding_constraint | solution.py:13
  395.7 0.0 copy-done.6
  395.7 0.1 copy.4
  395.9 0.0 copy-done.3
  395.9 2.4 fusion.39
  398.3 0.8 copy.8
  399.2 115.4 %all-to-all-done.1 = bf16[1,1,16,1,80,3072]{5,4,3,1,0,2:T(8,128)(2,1)} async-done(((bf16[1,1,16,1,80,3072]{5,4,3,1,0,2:T(8,128)(2,1)}), bf16[1,1,16,1,80,3072]{5,4,3,1,0,2:T(8,128)(2,1)}, u32[]{:S(2)}, u32[]{:S(2)}) %all-to-all-start.1) | async-done | bytes 7864352 | tf_op jit(solution)/sharding_constraint;jit(solution)/sharding_constraint | solution.py:13
  514.6 6.6 %fusion.27 = bf16[1,1,256,3072]{3,2,1,0:T(8,128)(2,1)} fusion(bf16[1,1,16,1,80,3072]{5,4,3,1,0,2:T(8,128)(2,1)} %all-to-all-done.1, bf16[256,16,80]{0,2,1:T(8,128)(2,1)S(1)} %copy.8), kind=kOutput, calls=%fused_computation.22 | convolution fusion | flops 2014052352 | bytes 10092544 | tf_op jit(solution)/abtec,aebcd->abtd/dot_general | solution.py:8
  (6 shorter events, 0.0 us)
Async XLA Ops:
  0.0 5.3 %copy-start = (bf16[1,1,256,3072]{3,2,1,0:T(8,128)(2,1)S(1)}, bf16[1,1,256,3072]{3,2,1,0:T(8,128)(2,1)}, u32[]{:S(2)}) copy-start(bf16[1,1,256,3072]{3,2,1,0:T(8,128)(2,1)} %param.3) | copy-start | bytes 4718596
  0.9 0.9 copy-start.2
  1.8 0.7 copy-start.4
  294.1 101.6 %copy-start.6 = (f32[1,1,256,4]{2,3,1,0:T(4,128)S(1)}, f32[1,1,256,4]{2,3,1,0:T(4,128)}, u32[]{:S(2)}) copy-start(f32[1,1,256,4]{2,3,1,0:T(4,128)} %param.1) | copy-start | bytes 12292
  294.1 101.8 %copy-start.3 = (s32[256,4]{1,0:T(8,128)S(1)}, s32[256,4]{1,0:T(8,128)}, u32[]{:S(2)}) copy-start(s32[256,4]{1,0:T(8,128)} %copy-done.2) | copy-start | bytes 12292
  294.1 101.8 %copy-start.5 = (s32[256,4]{1,0:T(8,128)S(1)}, s32[256,4]{1,0:T(8,128)}, u32[]{:S(2)}) copy-start(s32[256,4]{1,0:T(8,128)} %copy-done.4) | copy-start | bytes 12292
  294.1 227.1 %copy-start.1 = (bf16[1,1,256,3072]{3,2,1,0:T(8,128)(2,1)S(1)}, bf16[1,1,256,3072]{3,2,1,0:T(8,128)(2,1)}, u32[]{:S(2)}) copy-start(bf16[1,1,256,3072]{3,2,1,0:T(8,128)(2,1)} %param.3) | copy-start | bytes 4718596
  389.9 124.7 %all-to-all-start.1 = ((bf16[1,1,16,1,80,3072]{5,4,3,1,0,2:T(8,128)(2,1)}), bf16[1,1,16,1,80,3072]{5,4,3,1,0,2:T(8,128)(2,1)}, u32[]{:S(2)}, u32[]{:S(2)}) async-start(bf16[1,1,16,1,80,3072]{5,4,3,1,0,2:T(8,128)(2,1)} %convert_bitcast_fusion), calls=%async_computation.1 | async-start | bytes 15728640 | tf_op jit(solution)/sharding_constraint;jit(solution)/sharding_constraint | solution.py:13
where the time goes:
time: 521 us
  matrix products  305 us (59%)
  waiting for transfers between devices  115 us (22%)
  blocking collectives  90.8 us (17%)
  starting transfers between devices  5.81 us (1%)
    dot_general x7, matrix products, einsum(): return jnp.einsum(form, a.astype(jnp.float32), b.astype(jnp.float32))  305 us
    another operation x1, waiting for transfers between devices, placed(): return lax.with_sharding_constraint(v, NamedSharding(mesh, P(*spec)))  115 us
    another operation x1, blocking collectives, placed(): return lax.with_sharding_constraint(v, NamedSharding(mesh, P(*spec)))  90.8 us
  transfers between devices with their start and end apart: 1, of which 1 were waited for; matrix products, arithmetic and copies ran while one was open for 1% of the time, Pallas kernels for 0%

commit v1 on v0

v1 whole, which is shorter than its diff:
```python
import functools

import jax
import jax.numpy as jnp
from jax import lax
from jax.experimental import pallas as pl
from jax.experimental.pallas import tpu as pltpu
from jax.sharding import PartitionSpec as P

MESH = pl.DeviceIdType.MESH
PASSES = ((0, 1, 8, 4, 2), (12, 10, 6, 13, 11, 7, 14), (9, 5, 3, 15))
ORDER = tuple(k for group in PASSES for k in group)
TF, TN = 512, 256
N1, N2 = 3, 3


def flip(me, k):
    to = me
    for b in range(4):
        if (k >> b) & 1:
            to = to + (1 << b) * (1 - 2 * lax.rem(lax.div(me, 1 << b), 2))
    return to


def kernel(slots, z_in, wg, wu, wd, ret, z, h, w1g, w1u, w2, zsend, zrecv, s1, s2, rsend, rrecv):
    me = lax.axis_index("ep")
    depth, ff = wg.shape
    n_ff, n_d, n_pass = ff // TF, depth // TN, len(PASSES)

    def rows(pos):
        return pl.ds(pos * slots, slots)

    def peer(k):
        return {"ep": flip(me, k)}

    def block_in(pos):
        k = ORDER[pos]
        if k == 0:
            return pltpu.make_async_copy(z_in.at[rows(pos)], z.at[rows(pos)], zrecv.at[pos])
        return pltpu.make_async_remote_copy(
            z_in.at[rows(pos)], z.at[rows(pos)], zsend.at[pos], zrecv.at[pos], device_id=peer(k), device_id_type=MESH
        )

    def block_out(pos, columns=None):
        k = ORDER[pos]
        here = (rows(pos),) if columns is None else (rows(pos), columns)
        if k == 0:
            return pltpu.make_async_copy(z.at[here], ret.at[here], rrecv.at[pos])
        return pltpu.make_async_remote_copy(
            z.at[here], ret.at[here], rsend.at[pos], rrecv.at[pos], device_id=peer(k), device_id_type=MESH
        )

    def up_tiles(i):
        tile, slot = lax.rem(i, n_ff), lax.rem(i, N1)
        columns = pl.ds(pl.multiple_of(tile * TF, TF), TF)
        return (
            pltpu.make_async_copy(wg.at[:, columns], w1g.at[slot], s1.at[0, slot]),
            pltpu.make_async_copy(wu.at[:, columns], w1u.at[slot], s1.at[1, slot]),
        )

    def down_tile(j):
        tile, slot = lax.rem(j, n_d), lax.rem(j, N2)
        columns = pl.ds(pl.multiple_of(tile * TN, TN), TN)
        return pltpu.make_async_copy(wd.at[:, columns], w2.at[slot], s2.at[slot])

    for pos in range(len(ORDER)):
        block_in(pos).start()
    for i in range(N1 - 1):
        for copy in up_tiles(i):
            copy.start()
    for j in range(N2 - 1):
        down_tile(j).start()

    first = 0
    for p, group in enumerate(PASSES):
        last = p == n_pass - 1
        here = range(first, first + len(group))
        start, size = first * slots, len(group) * slots
        for pos in here:
            if ORDER[pos] == 0:
                block_in(pos).wait()
            else:
                block_in(pos).wait_recv()

        def up(t, carry, p=p, start=start, size=size):
            i = p * n_ff + t

            @pl.when(i + N1 - 1 < n_pass * n_ff)
            def _():
                for copy in up_tiles(i + N1 - 1):
                    copy.start()

            for copy in up_tiles(i):
                copy.wait()
            slot = lax.rem(i, N1)
            for n in range(0, TF, 256):
                rhs = z[pl.ds(start, size), :]
                g = jnp.dot(rhs, w1g[slot, :, n : n + 256], preferred_element_type=jnp.float32)
                u = jnp.dot(rhs, w1u[slot, :, n : n + 256], preferred_element_type=jnp.float32)
                columns = pl.ds(pl.multiple_of(t * TF + n, 256), 256)
                h[pl.ds(0, size), columns] = (jax.nn.silu(g) * u).astype(jnp.bfloat16)
            return carry

        lax.fori_loop(0, n_ff, up, 0)

        def down(n, carry, p=p, start=start, size=size, here=here, last=last):
            j = p * n_d + n

            @pl.when(j + N2 - 1 < n_pass * n_d)
            def _():
                down_tile(j + N2 - 1).start()

            if last:

                @pl.when(n > 0)
                def _():
                    for pos in here:
                        block_out(pos, pl.ds(pl.multiple_of((n - 1) * TN, TN), TN)).start()

            down_tile(j).wait()
            slot = lax.rem(j, N2)
            out = jnp.dot(h[pl.ds(0, size), :], w2[slot], preferred_element_type=jnp.float32)
            z[pl.ds(start, size), pl.ds(pl.multiple_of(n * TN, TN), TN)] = out.astype(jnp.bfloat16)
            return carry

        lax.fori_loop(0, n_d, down, 0)
        for pos in here:
            if last:
                block_out(pos, pl.ds((n_d - 1) * TN, TN)).start()
            else:
                block_out(pos).start()
        first += len(group)

    for pos in range(len(ORDER)):
        if ORDER[pos] == 0:
            block_out(pos).wait()
        else:
            block_in(pos).wait_send()
            block_out(pos).wait()


def solution(mesh):
    def step(x, expert, slot, gate, w_gate, w_up, w_down):
        tokens, top = expert.shape[2:]
        depth, ff = w_gate.shape[1:]
        experts = mesh.shape["ep"]
        slots = 5 * tokens * top // (4 * experts)
        held = experts * slots
        me = lax.axis_index("ep")
        x, expert, slot, gate = x[0, 0], expert[0, 0].T, slot[0, 0].T, gate[0, 0].T
        apart = jnp.bitwise_xor(expert, me)
        place = sum(jnp.where(apart == k, pos, 0) for pos, k in enumerate(ORDER))
        row = jnp.where(slot < slots, place * slots + slot, -1)
        at = lax.broadcasted_iota(jnp.int32, (held, tokens), 0)
        hit = [at == row[j][None, :] for j in range(top)]
        dispatch = functools.reduce(jnp.logical_or, hit).astype(jnp.bfloat16)
        weight = gate.astype(jnp.bfloat16).astype(jnp.float32)
        combine = sum(jnp.where(hit[j], weight[j][None, :], 0.0) for j in range(top)).astype(jnp.bfloat16)
        z = jnp.dot(dispatch, x, preferred_element_type=jnp.float32).astype(jnp.bfloat16)
        most = max(len(group) for group in PASSES) * slots
        n = len(ORDER)
        ret = pl.pallas_call(
            functools.partial(kernel, slots),
            out_shape=jax.ShapeDtypeStruct((held, depth), jnp.bfloat16),
            in_specs=[pl.BlockSpec(memory_space=pl.ANY)] * 4,
            out_specs=pl.BlockSpec(memory_space=pl.ANY),
            scratch_shapes=[
                pltpu.VMEM((held, depth), jnp.bfloat16),
                pltpu.VMEM((most, ff), jnp.bfloat16),
                pltpu.VMEM((N1, depth, TF), jnp.bfloat16),
                pltpu.VMEM((N1, depth, TF), jnp.bfloat16),
                pltpu.VMEM((N2, ff, TN), jnp.bfloat16),
                pltpu.SemaphoreType.DMA((n,)),
                pltpu.SemaphoreType.DMA((n,)),
                pltpu.SemaphoreType.DMA((2, N1)),
                pltpu.SemaphoreType.DMA((N2,)),
                pltpu.SemaphoreType.DMA((n,)),
                pltpu.SemaphoreType.DMA((n,)),
            ],
            compiler_params=pltpu.CompilerParams(vmem_limit_bytes=67043328, has_side_effects=True),
        )(z, w_gate[0], w_up[0], w_down[0])
        y = lax.dot_general(combine, ret, (((0,), (0,)), ((), ())), preferred_element_type=jnp.float32)
        return y.astype(jnp.bfloat16)[None, None]

    block = P("dp", "ep", None, None)
    weights = P("ep", None, None)
    return jax.shard_map(
        step, mesh=mesh, in_specs=(block,) * 4 + (weights,) * 3, out_specs=block, check_vma=False
    )
```

time: 521 us -> 327 us (0.63)
  the two profiles are of different devices: /device:TPU:13 before, /device:TPU:1 now
where the time goes in v1:
time: 327 us; the launch traced here: 326 us
  Pallas kernels  311 us (95%)
  matrix products  13.9 us (4%)
    pallas_call x1, Pallas kernels, step(): pl.pallas_call(functools.partial(kernel, slots), out_shape=jax.ShapeDtype...  311 us
    dot_general x1, matrix products, step(): lax.dot_general(combine, ret, (((0,), (0,)), ((), ())), preferred_element...  7 us
    dot_general x1, matrix products, step(): jnp.dot(dispatch, x, preferred_element_type=jnp.float32)  6.93 us

profile of v1, /device:TPU:1, one launch (start us, length us, event | category | flops | bytes accessed | tf_op | source)
XLA Modules:
  0.0 326.1 jit_solution(14793882023665877369)
XLA Ops:
  0.0 0.7 fusion.21
  0.7 0.0 copy-start
  0.8 0.0 copy-start.1
  0.8 0.0 copy-start.2
  0.8 0.0 copy-start.3
  0.8 6.9 %convolution_convert_fusion.z_in = bf16[1280,3072]{1,0:T(8,128)(2,1)} fusion(bf16[1,1,256,3072]{3,2,1,0:T(8,128)(2,1)} %param.7, s32[256]{0:T(256)S(1)} %bitcast.52, s32[256]{0:T(256)S(1)} %bitcast.54, s32[256]{0:T(256)S(1)} %bitcast.56, s32[256]{0:T(256)S(1)} %bitcast.50), kind=kOutput, calls=%fused_computation | convolution fusion | flops 2019491840 | bytes 9441280 | tf_op jit(solution)/shard_map/dot_general | solution.py:159
  7.7 0.0 copy-done
  7.7 0.0 copy-done.1
  7.7 0.0 copy-done.2
  7.7 0.0 copy-done.3
  7.7 310.7 %shard_map.73 = bf16[1280,3072]{1,0:T(8,128)(2,1)} custom-call(bf16[1280,3072]{1,0:T(8,128)(2,1)} %convolution_convert_fusion.z_in, bf16[3072,10752]{1,0:T(8,128)(2,1)} %bitcast.47, bf16[3072,10752]{1,0:T(8,128)(2,1)} %bitcast.48, bf16[10752,3072]{1,0:T(8,128)(2,1)} %bitcast.49), custom_call_target="tpu_custom_call" | custom-call | tf_op jit(solution)/shard_map/pallas_call | solution.py:162
  318.4 0.7 convert_bitcast_fusion
  319.1 7.0 %fusion = bf16[1,1,256,3072]{3,2,1,0:T(8,128)(2,1)} fusion(bf16[1280,3072]{1,0:T(8,128)(2,1)} %shard_map.73, f32[256]{0:T(256)S(1)} %bitcast.59, s32[256]{0:T(256)} %bitcast.53, f32[256]{0:T(256)S(1)} %bitcast.60, s32[256]{0:T(256)} %bitcast.55, f32[256]{0:T(256)S(1)} %bitcast.61, s32[256]{0:T(256)} %bitcast.57, f32[256]{0:T(256)S(1)} %bitcast.58, ...), kind=kOutput, calls=%fused_computation.2 | convolution fusion | flops 2017984512 | bytes 9445376 | tf_op jit(solution)/shard_map/dot_general | solution.py:182
  (2 shorter events, 0.0 us)
Async XLA Ops:
  0.7 7.0 %copy-start = (s32[1,256]{1,0:T(1,128)}, s32[1,256]{1,0:T(1,128)S(1)}, u32[]{:S(2)}) copy-start(s32[1,256]{1,0:T(1,128)S(1)} %get-tuple-element.9) | copy-start | bytes 3076
  0.8 7.0 %copy-start.1 = (s32[1,256]{1,0:T(1,128)}, s32[1,256]{1,0:T(1,128)S(1)}, u32[]{:S(2)}) copy-start(s32[1,256]{1,0:T(1,128)S(1)} %get-tuple-element.10) | copy-start | bytes 3076
  0.8 7.0 %copy-start.2 = (s32[1,256]{1,0:T(1,128)}, s32[1,256]{1,0:T(1,128)S(1)}, u32[]{:S(2)}) copy-start(s32[1,256]{1,0:T(1,128)S(1)} %get-tuple-element.11) | copy-start | bytes 3076
  0.8 7.0 %copy-start.3 = (s32[1,256]{1,0:T(1,128)}, s32[1,256]{1,0:T(1,128)S(1)}, u32[]{:S(2)}) copy-start(s32[1,256]{1,0:T(1,128)S(1)} %get-tuple-element.12) | copy-start | bytes 3076

commit v2 on v1

--- a/solution.py
+++ b/solution.py
@@ -8,8 +8,10 @@
 from jax.sharding import PartitionSpec as P
 
 MESH = pl.DeviceIdType.MESH
-PASSES = ((0, 1, 8, 4, 2), (12, 10, 6, 13, 11, 7, 14), (9, 5, 3, 15))
+PASSES = ((1, 8, 4, 2), (12, 10, 6, 13, 11, 7, 15), (0, 9, 5, 3, 14))
 ORDER = tuple(k for group in PASSES for k in group)
+SENDS = ({0: (12, 10, 6), 9: (13, 11, 7), 17: (15,)}, {1: (9, 5, 3), 6: (14,)}, {})
+RETURNS = ({}, {0: (1, 8, 4, 2)}, {0: (12, 10, 6), 8: (13, 11, 7), 16: (15,)})
 TF, TN = 512, 256
 N1, N2 = 3, 3
 
@@ -22,10 +24,11 @@
     return to
 
 
-def kernel(slots, z_in, wg, wu, wd, ret, z, h, w1g, w1u, w2, zsend, zrecv, s1, s2, rsend, rrecv):
+def kernel(slots, x, row, wg, wu, wd, ret, z, h, late, w1g, w1u, w2, zsend, zrecv, s1, s2, rsend, rrecv):
     me = lax.axis_index("ep")
     depth, ff = wg.shape
     n_ff, n_d, n_pass = ff // TF, depth // TN, len(PASSES)
+    n_a, n_b = len(PASSES[0]), len(PASSES[1])
 
     def rows(pos):
         return pl.ds(pos * slots, slots)
@@ -33,12 +36,30 @@
     def peer(k):
         return {"ep": flip(me, k)}
 
+    def staged(pos, column=0, width=None):
+        width = depth if width is None else width
+        if ORDER[pos] == 0:
+            return z.at[rows(pos), pl.ds(column, width)]
+        if pos < n_a:
+            return h.at[rows(pos), pl.ds(column, width)]
+        if pos < n_a + n_b:
+            at = pos - n_a
+            return h.at[rows(n_a + at // 3), pl.ds((at % 3) * depth + column, width)]
+        return late.at[rows(pos - n_a - n_b - 1), pl.ds(column, width)]
+
+    def fill(first, count):
+        at = lax.broadcasted_iota(jnp.int32, (count * slots, row.shape[1]), 0) + first * slots
+        hit = functools.reduce(jnp.logical_or, [at == row[j : j + 1, :] for j in range(row.shape[0])])
+        pick = jnp.where(hit, 1.0, 0.0).astype(jnp.bfloat16)
+        for column in range(0, depth, 256):
+            block = jnp.dot(pick, x[:, column : column + 256], preferred_element_type=jnp.float32)
+            block = block.astype(jnp.bfloat16)
+            for i in range(count):
+                staged(first + i, column, 256)[...] = block[i * slots : (i + 1) * slots]
+
     def block_in(pos):
-        k = ORDER[pos]
-        if k == 0:
-            return pltpu.make_async_copy(z_in.at[rows(pos)], z.at[rows(pos)], zrecv.at[pos])
         return pltpu.make_async_remote_copy(
-            z_in.at[rows(pos)], z.at[rows(pos)], zsend.at[pos], zrecv.at[pos], device_id=peer(k), device_id_type=MESH
+            staged(pos), z.at[rows(pos)], zsend.at[pos], zrecv.at[pos], device_id=peer(ORDER[pos]), device_id_type=MESH
         )
 
     def block_out(pos, columns=None):
@@ -63,13 +84,16 @@
         columns = pl.ds(pl.multiple_of(tile * TN, TN), TN)
         return pltpu.make_async_copy(wd.at[:, columns], w2.at[slot], s2.at[slot])
 
-    for pos in range(len(ORDER)):
-        block_in(pos).start()
     for i in range(N1 - 1):
         for copy in up_tiles(i):
             copy.start()
     for j in range(N2 - 1):
         down_tile(j).start()
+    fill(0, n_a)
+    for pos in range(n_a):
+        block_in(pos).start()
+    fill(n_a, n_b)
+    fill(n_a + n_b, len(ORDER) - n_a - n_b)
 
     first = 0
     for p, group in enumerate(PASSES):
@@ -77,10 +101,10 @@
         here = range(first, first + len(group))
         start, size = first * slots, len(group) * slots
         for pos in here:
-            if ORDER[pos] == 0:
-                block_in(pos).wait()
-            else:
+            if ORDER[pos] != 0:
                 block_in(pos).wait_recv()
+                if not last:
+                    block_in(pos).wait_send()
 
         def up(t, carry, p=p, start=start, size=size):
             i = p * n_ff + t
@@ -92,6 +116,20 @@
 
             for copy in up_tiles(i):
                 copy.wait()
+            for at, blocks in SENDS[p].items():
+
+                @pl.when(t == at)
+                def _(blocks=blocks):
+                    for k in blocks:
+                        block_in(ORDER.index(k)).start()
+
+            for at, blocks in RETURNS[p].items():
+
+                @pl.when(t == at)
+                def _(blocks=blocks):
+                    for k in blocks:
+                        block_out(ORDER.index(k)).start()
+
             slot = lax.rem(i, N1)
             for n in range(0, TF, 256):
                 rhs = z[pl.ds(start, size), :]
@@ -124,18 +162,17 @@
             return carry
 
         lax.fori_loop(0, n_d, down, 0)
-        for pos in here:
-            if last:
+        if last:
+            for pos in here:
                 block_out(pos, pl.ds((n_d - 1) * TN, TN)).start()
-            else:
-                block_out(pos).start()
         first += len(group)
 
     for pos in range(len(ORDER)):
         if ORDER[pos] == 0:
             block_out(pos).wait()
         else:
-            block_in(pos).wait_send()
+            if pos >= n_a + n_b:
+                block_in(pos).wait_send()
             block_out(pos).wait()
 
 
@@ -153,20 +190,19 @@
         row = jnp.where(slot < slots, place * slots + slot, -1)
         at = lax.broadcasted_iota(jnp.int32, (held, tokens), 0)
         hit = [at == row[j][None, :] for j in range(top)]
-        dispatch = functools.reduce(jnp.logical_or, hit).astype(jnp.bfloat16)
         weight = gate.astype(jnp.bfloat16).astype(jnp.float32)
         combine = sum(jnp.where(hit[j], weight[j][None, :], 0.0) for j in range(top)).astype(jnp.bfloat16)
-        z = jnp.dot(dispatch, x, preferred_element_type=jnp.float32).astype(jnp.bfloat16)
         most = max(len(group) for group in PASSES) * slots
         n = len(ORDER)
         ret = pl.pallas_call(
             functools.partial(kernel, slots),
             out_shape=jax.ShapeDtypeStruct((held, depth), jnp.bfloat16),
-            in_specs=[pl.BlockSpec(memory_space=pl.ANY)] * 4,
+            in_specs=[pl.BlockSpec(memory_space=pltpu.VMEM)] * 2 + [pl.BlockSpec(memory_space=pl.ANY)] * 3,
             out_specs=pl.BlockSpec(memory_space=pl.ANY),
             scratch_shapes=[
                 pltpu.VMEM((held, depth), jnp.bfloat16),
                 pltpu.VMEM((most, ff), jnp.bfloat16),
+                pltpu.VMEM(((len(PASSES[-1]) - 1) * slots, depth), jnp.bfloat16),
                 pltpu.VMEM((N1, depth, TF), jnp.bfloat16),
                 pltpu.VMEM((N1, depth, TF), jnp.bfloat16),
                 pltpu.VMEM((N2, ff, TN), jnp.bfloat16),
@@ -178,7 +214,7 @@
                 pltpu.SemaphoreType.DMA((n,)),
             ],
             compiler_params=pltpu.CompilerParams(vmem_limit_bytes=67043328, has_side_effects=True),
-        )(z, w_gate[0], w_up[0], w_down[0])
+        )(x, row, w_gate[0], w_up[0], w_down[0])
         y = lax.dot_general(combine, ret, (((0,), (0,)), ((), ())), preferred_element_type=jnp.float32)
         return y.astype(jnp.bfloat16)[None, None]
 

time: 327 us -> 316 us (0.966)
  matrix products: 13.9 us -> 7.03 us
  Pallas kernels: 311 us -> 307 us
    dot_general x1 -> x0, matrix products: 6.93 us -> none  [step(): jnp.dot(dispatch, x, preferred_element_type=jnp.float32)]
    pallas_call x1, Pallas kernels: 311 us -> 307 us  [step(): pl.pallas_call(functools.partial(kernel, slots), out_shape=jax.ShapeDtype...]
where the time goes in v2:
time: 316 us
  Pallas kernels  307 us (97%)
  matrix products  7.03 us (2%)
    pallas_call x1, Pallas kernels, step(): pl.pallas_call(functools.partial(kernel, slots), out_shape=jax.ShapeDtype...  307 us
    dot_general x1, matrix products, step(): lax.dot_general(combine, ret, (((0,), (0,)), ((), ())), preferred_element...  7.03 us

profile of v2, /device:TPU:1, one launch (start us, length us, event | category | flops | bytes accessed | tf_op | source)
XLA Modules:
  0.0 316.2 jit_solution(17510182516685453224)
XLA Ops:
  0.0 0.7 fusion.12.row
  0.7 0.0 copy-start
  0.7 0.7 convert_bitcast_fusion
  1.4 0.6 fusion.15
  2.0 0.0 copy-done
  2.0 0.6 fusion.14
  2.6 306.5 %shard_map.73 = bf16[1280,3072]{1,0:T(8,128)(2,1)} custom-call(bf16[256,3072]{1,0:T(8,128)(2,1)} %bitcast.48, s32[4,256]{1,0:T(4,128)} %copy-done, bf16[3072,10752]{1,0:T(8,128)(2,1)} %bitcast.45, bf16[3072,10752]{1,0:T(8,128)(2,1)} %bitcast.46, bf16[10752,3072]{1,0:T(8,128)(2,1)} %bitcast.47), custom_call_target="tpu_custom_call" | custom-call | tf_op jit(solution)/shard_map/pallas_call | solution.py:197
  309.2 7.0 %fusion = bf16[1,1,256,3072]{3,2,1,0:T(8,128)(2,1)} fusion(bf16[1280,3072]{1,0:T(8,128)(2,1)} %shard_map.73, f32[256]{0:T(256)} %bitcast.50, s32[256]{0:T(256)} %bitcast.54, f32[256]{0:T(256)} %bitcast.51, s32[256]{0:T(256)} %bitcast.55, f32[256]{0:T(256)} %bitcast.52, s32[256]{0:T(256)} %bitcast.56, f32[256]{0:T(256)} %bitcast.49, s32[256]{0:T(256)} %bitcast.53), kind=kOutput, calls=%fused_computation.1 | convolution fusion | flops 2017984512 | bytes 9445376 | tf_op jit(solution)/shard_map/dot_general | solution.py:218
Async XLA Ops:
  0.7 1.3 copy-start

commit v3 on v2

v3 whole, which is shorter than its diff:
```python
import functools

import jax
import jax.numpy as jnp
from jax import lax
from jax.experimental import pallas as pl
from jax.experimental.pallas import tpu as pltpu
from jax.sharding import PartitionSpec as P

MESH = pl.DeviceIdType.MESH
SLOTS, CUT = 80, 48
PASSES = (
    ((0, 0, SLOTS), (1, 0, SLOTS), (8, 0, CUT), (4, 0, CUT), (2, 0, CUT)),
    tuple((k, 0, SLOTS) for k in (12, 10, 6, 14, 15)) + tuple((k, CUT, SLOTS) for k in (8, 4, 2)),
    tuple((k, 0, SLOTS) for k in (9, 5, 3, 13, 11, 7)),
)
PIECES = tuple(piece for group in PASSES for piece in group)
SIZES = tuple(stop - start for _, start, stop in PIECES)
STARTS = tuple(sum(SIZES[:i]) for i in range(len(PIECES)))
TF, TN = 512, 256
N1, N2 = 3, 3


def flip(me, k):
    to = me
    for b in range(4):
        if (k >> b) & 1:
            to = to + (1 << b) * (1 - 2 * lax.rem(lax.div(me, 1 << b), 2))
    return to


def kernel(x, row, gate, wg, wu, wd, ret, weights, z, h, late, pick, w1g, w1u, w2, zsend, zrecv, s1, s2, rsend, rrecv, s3):
    me = lax.axis_index("ep")
    depth, ff = wg.shape
    n_ff, n_d, n_pass = ff // TF, depth // TN, len(PASSES)
    n_a, n_b = len(PASSES[0]), len(PASSES[1])
    row_b, row_c = STARTS[n_a], STARTS[n_a + n_b]

    def rows(pos):
        return pl.ds(STARTS[pos], SIZES[pos])

    def peer(k):
        return {"ep": flip(me, k)}

    def staged(pos, column=0, width=None):
        width = depth if width is None else width
        if PIECES[pos][0] == 0:
            return z.at[rows(pos), pl.ds(column, width)]
        if pos < n_a:
            return h.at[rows(pos), pl.ds(column, width)]
        if pos < n_a + n_b:
            whole = sum(size == SLOTS for size in SIZES[n_a : n_a + n_b])
            at = pos - n_a
            first = row_b + at // 3 * SLOTS if at < whole else row_b + -(-whole // 3) * SLOTS
            column += (at if at < whole else at - whole) % 3 * depth
            return h.at[pl.ds(first, SIZES[pos]), pl.ds(column, width)]
        return late.at[pl.ds(STARTS[pos] - row_c, SIZES[pos]), pl.ds(column, width)]

    def hits(first, count):
        at = lax.broadcasted_iota(jnp.int32, (count, row.shape[1]), 0) + first
        return [at == row[j : j + 1, :] for j in range(row.shape[0])]

    def fill(first, count):
        top, total = STARTS[first], sum(SIZES[first : first + count])
        chosen = jnp.where(functools.reduce(jnp.logical_or, hits(top, total)), 1.0, 0.0).astype(jnp.bfloat16)
        for column in range(0, depth, 256):
            block = jnp.dot(chosen, x[:, column : column + 256], preferred_element_type=jnp.float32)
            block = block.astype(jnp.bfloat16)
            for pos in range(first, first + count):
                staged(pos, column, 256)[...] = block[STARTS[pos] - top : STARTS[pos] - top + SIZES[pos]]

    def block_in(pos):
        return pltpu.make_async_remote_copy(
            staged(pos), z.at[rows(pos)], zsend.at[pos], zrecv.at[pos], device_id=peer(PIECES[pos][0]), device_id_type=MESH
        )

    def block_out(pos, columns=None):
        k = PIECES[pos][0]
        here = (rows(pos),) if columns is None else (rows(pos), columns)
        if k == 0:
            return pltpu.make_async_copy(z.at[here], ret.at[here], rrecv.at[pos])
        return pltpu.make_async_remote_copy(
            z.at[here], ret.at[here], rsend.at[pos], rrecv.at[pos], device_id=peer(k), device_id_type=MESH
        )

    def up_tiles(i):
        tile, slot = lax.rem(i, n_ff), lax.rem(i, N1)
        columns = pl.ds(pl.multiple_of(tile * TF, TF), TF)
        return (
            pltpu.make_async_copy(wg.at[:, columns], w1g.at[slot], s1.at[0, slot]),
            pltpu.make_async_copy(wu.at[:, columns], w1u.at[slot], s1.at[1, slot]),
        )

    def down_tile(j):
        tile, slot = lax.rem(j, n_d), lax.rem(j, N2)
        columns = pl.ds(pl.multiple_of(tile * TN, TN), TN)
        return pltpu.make_async_copy(wd.at[:, columns], w2.at[slot], s2.at[slot])

    for i in range(N1 - 1):
        for copy in up_tiles(i):
            copy.start()
    for j in range(N2 - 1):
        down_tile(j).start()
    fill(0, n_a)
    for pos in range(n_a):
        if PIECES[pos][0] != 0:
            block_in(pos).start()
    fill(n_a, n_b)
    fill(n_a + n_b, len(PIECES) - n_a - n_b)
    half = z.shape[0] // 2
    for top in (0, half):
        weight = sum(jnp.where(hit, gate[j : j + 1, :], 0.0) for j, hit in enumerate(hits(top, half)))
        pick[:, pl.ds(top, half)] = weight.T.astype(jnp.bfloat16)
    combine = pltpu.make_async_copy(pick, weights, s3)
    combine.start()

    first, before = 0, ()
    for p, group in enumerate(PASSES):
        last = p == n_pass - 1
        here = range(first, first + len(group))
        start, size = STARTS[first], sum(SIZES[first : first + len(group)])
        for pos in here:
            if PIECES[pos][0] != 0:
                block_in(pos).wait_recv()
                if not last:
                    block_in(pos).wait_send()

        if p == 0:
            for pos in range(n_a, len(PIECES)):
                if PIECES[pos][0] != 0:
                    block_in(pos).start()
        else:
            for pos in before:
                block_out(pos).start()
        before = here

        def up(t, carry, p=p, start=start, size=size):
            i = p * n_ff + t

            @pl.when(i + N1 - 1 < n_pass * n_ff)
            def _():
                for copy in up_tiles(i + N1 - 1):
                    copy.start()

            for copy in up_tiles(i):
                copy.wait()
            slot = lax.rem(i, N1)
            for n in range(0, TF, 256):
                rhs = z[pl.ds(start, size), :]
                g = jnp.dot(rhs, w1g[slot, :, n : n + 256], preferred_element_type=jnp.float32)
                u = jnp.dot(rhs, w1u[slot, :, n : n + 256], preferred_element_type=jnp.float32)
                columns = pl.ds(pl.multiple_of(t * TF + n, 256), 256)
                h[pl.ds(0, size), columns] = (jax.nn.silu(g) * u).astype(jnp.bfloat16)
            return carry

        lax.fori_loop(0, n_ff, up, 0)

        def down(n, carry, p=p, start=start, size=size, here=here, last=last):
            j = p * n_d + n

            @pl.when(j + N2 - 1 < n_pass * n_d)
            def _():
                down_tile(j + N2 - 1).start()

            if last:

                @pl.when(n > 0)
                def _():
                    for pos in here:
                        block_out(pos, pl.ds(pl.multiple_of((n - 1) * TN, TN), TN)).start()

            down_tile(j).wait()
            slot = lax.rem(j, N2)
            out = jnp.dot(h[pl.ds(0, size), :], w2[slot], preferred_element_type=jnp.float32)
            z[pl.ds(start, size), pl.ds(pl.multiple_of(n * TN, TN), TN)] = out.astype(jnp.bfloat16)
            return carry

        lax.fori_loop(0, n_d, down, 0)
        if last:
            for pos in here:
                block_out(pos, pl.ds((n_d - 1) * TN, TN)).start()
        first += len(group)

    combine.wait()
    for pos in range(len(PIECES)):
        if PIECES[pos][0] == 0:
            block_out(pos).wait()
        else:
            if pos >= n_a + n_b:
                block_in(pos).wait_send()
            block_out(pos).wait()


def add_up(combine, ret, y):
    y[...] = jnp.dot(combine[...], ret[...], preferred_element_type=jnp.float32).astype(y.dtype)


def solution(mesh):
    def step(x, expert, slot, gate, w_gate, w_up, w_down):
        tokens, top = expert.shape[2:]
        depth, ff = w_gate.shape[1:]
        experts = mesh.shape["ep"]
        slots = 5 * tokens * top // (4 * experts)
        held = experts * slots
        me = lax.axis_index("ep")
        x, expert, slot, gate = x[0, 0], expert[0, 0].T, slot[0, 0].T, gate[0, 0].T
        apart = jnp.bitwise_xor(expert, me)
        row = jnp.full(slot.shape, -1, jnp.int32)
        for (k, start, stop), first in zip(PIECES, STARTS):
            row = jnp.where((apart == k) & (slot >= start) & (slot < stop), slot - start + first, row)
        weight = gate.astype(jnp.bfloat16).astype(jnp.float32)
        assert slots == SLOTS and held == sum(SIZES)
        most = max(sum(stop - start for _, start, stop in group) for group in PASSES)
        n = len(PIECES)
        ret, combine = pl.pallas_call(
            kernel,
            out_shape=(
                jax.ShapeDtypeStruct((held, depth), jnp.bfloat16),
                jax.ShapeDtypeStruct((tokens, held), jnp.bfloat16),
            ),
            in_specs=[pl.BlockSpec(memory_space=pltpu.VMEM)] * 3 + [pl.BlockSpec(memory_space=pl.ANY)] * 3,
            out_specs=(pl.BlockSpec(memory_space=pl.ANY),) * 2,
            scratch_shapes=[
                pltpu.VMEM((held, depth), jnp.bfloat16),
                pltpu.VMEM((most, ff), jnp.bfloat16),
                pltpu.VMEM((held - STARTS[n - len(PASSES[-1])], depth), jnp.bfloat16),
                pltpu.VMEM((tokens, held), jnp.bfloat16),
                pltpu.VMEM((N1, depth, TF), jnp.bfloat16),
                pltpu.VMEM((N1, depth, TF), jnp.bfloat16),
                pltpu.VMEM((N2, ff, TN), jnp.bfloat16),
                pltpu.SemaphoreType.DMA((n,)),
                pltpu.SemaphoreType.DMA((n,)),
                pltpu.SemaphoreType.DMA((2, N1)),
                pltpu.SemaphoreType.DMA((N2,)),
                pltpu.SemaphoreType.DMA((n,)),
                pltpu.SemaphoreType.DMA((n,)),
                pltpu.SemaphoreType.DMA,
            ],
            compiler_params=pltpu.CompilerParams(vmem_limit_bytes=67043328, has_side_effects=True),
        )(x, row, weight, w_gate[0], w_up[0], w_down[0])
        width = depth // 4
        y = pl.pallas_call(
            add_up,
            out_shape=jax.ShapeDtypeStruct((tokens, depth), jnp.bfloat16),
            grid=(depth // width,),
            in_specs=[pl.BlockSpec((tokens, held), lambda n: (0, 0)), pl.BlockSpec((held, width), lambda n: (0, n))],
            out_specs=pl.BlockSpec((tokens, width), lambda n: (0, n)),
        )(combine, ret)
        return y[None, None]

    block = P("dp", "ep", None, None)
    weights = P("ep", None, None)
    return jax.shard_map(
        step, mesh=mesh, in_specs=(block,) * 4 + (weights,) * 3, out_specs=block, check_vma=False
    )
```

time: 316 us -> 306 us (0.968)
  matrix products: 7.03 us -> 0 us
  Pallas kernels: 307 us -> 303 us
    dot_general x1 -> x0, matrix products: 7.03 us -> none  [step(): lax.dot_general(combine, ret, (((0,), (0,)), ((), ())), preferred_element...]
    pallas_call x1 -> x2, Pallas kernels: 307 us -> 303 us  [the longest x1 297 us: step(): pl.pallas_call(kernel, out_shape=(jax.ShapeDtypeStruct((held, depth), jnp...]
where the time goes in v3:
time: 306 us
  Pallas kernels  303 us (99%)
    pallas_call x1, Pallas kernels, step(): pl.pallas_call(kernel, out_shape=(jax.ShapeDtypeStruct((held, depth), jnp...  297 us
    pallas_call x1, Pallas kernels, step(): pl.pallas_call(add_up, out_shape=jax.ShapeDtypeStruct((tokens, depth), jn...  6.38 us

profile of v3, /device:TPU:1, one launch (start us, length us, event | category | flops | bytes accessed | tf_op | source)
XLA Modules:
  0.0 305.5 jit_solution(10623216608574174190)
XLA Ops:
  0.0 1.3 fusion.row
  1.3 1.3 convert_bitcast_fusion.gate
  2.6 296.5 %shard_map.73 = (bf16[1280,3072]{1,0:T(8,128)(2,1)}, bf16[256,1280]{1,0:T(8,128)(2,1)}) custom-call(bf16[256,3072]{1,0:T(8,128)(2,1)} %bitcast.269, s32[4,256]{1,0:T(4,128)} %fusion.row, f32[4,256]{1,0:T(4,128)} %convert_bitcast_fusion.gate, bf16[3072,10752]{1,0:T(8,128)(2,1)} %bitcast.266, bf16[3072,10752]{1,0:T(8,128)(2,1)} %bitcast.267, ...), custom_call_target="tpu_custom_call" | custom-call | tf_op jit(solution)/shard_map/pallas_call | solution.py:215
  299.2 6.4 %shard_map.74 = bf16[256,3072]{1,0:T(8,128)(2,1)} custom-call(bf16[256,1280]{1,0:T(8,128)(2,1)} %get-tuple-element.7.combine, bf16[1280,3072]{1,0:T(8,128)(2,1)} %get-tuple-element.8.ret), custom_call_target="tpu_custom_call" | custom-call | tf_op jit(solution)/shard_map/pallas_call | solution.py:242
